TPU v7x, 32 devices: a whole 2x2x4 slice. The times are simulated.
32 devices in a mesh: clusters: 2 (over x), blk: 16 (over z, y, core).
Axes of the slice: x: 2, y: 2, z: 4, core: 2. Of those that a mesh axis runs over, the one named last changes fastest.
Arguments:
- positions: float32 [3, 65536], P(None, ('clusters', 'blk')), parts along dimension 1, may hold values from -6 to 6
- velocities: float32 [3, 65536], P(None, ('clusters', 'blk')), parts along dimension 1, may hold values from -6 to 6
- masses: float32 [65536], P(('clusters', 'blk')), parts along dimension 0, may hold values from 0.000390625 to 0.00390625
- active: int32 [8192], P(('clusters', 'blk')), parts along dimension 0, may hold values from 0 to 32767, as said below
Outputs:
- new_positions: float32 [3, 8192], P(None, ('clusters', 'blk')), parts along dimension 1
- new_velocities: float32 [3, 8192], P(None, ('clusters', 'blk')), parts along dimension 1
- accelerations: float32 [3, 8192], P(None, ('clusters', 'blk')), parts along dimension 1
- jerks: float32 [3, 8192], P(None, ('clusters', 'blk')), parts along dimension 1
There are 2 independent parts, one for each index of `clusters`. A program takes and returns all parts, laid end to end along the dimension named above; each array names one. Nothing has to cross between parts.
Inputs may be any that keep to these rules, and one draw needn't show every extreme that they name: Entries b * 256 to (b + 1) * 256 - 1 of active name distinct stars among b * 2048 to (b + 1) * 2048 - 1, for every block b.
All inputs are finite; a program needn't handle non-finite values.
Results may differ from a plain program's by a relative error of at most 0.00023.
Values sent between devices are 32-bit elements; how exact they have to be, the bound alone decides.
A program may use at most 64 MiB of HBM per device.

v0:
```python
import functools

import jax
import jax.numpy as jnp
from jax import lax
from jax.experimental import pallas as pl
from jax.experimental.pallas import tpu as pltpu
from jax.sharding import PartitionSpec as P

STEPS = 2
TIME_STEP = 0.03125
ROWS = 32
F32 = jnp.float32
BF16 = jnp.bfloat16


def split3(value):
    high = value.astype(BF16)
    rest = value - high.astype(F32)
    middle = rest.astype(BF16)
    low = (rest - middle.astype(F32)).astype(BF16)
    return [high, middle, low]


def kernel(
    n,
    pos_ref,
    vel_ref,
    mass_ref,
    idx_ref,
    out_ref,
    slots,
    target,
    total,
    send_sem,
    recv_sem,
):
    me = lax.axis_index("blk")
    act = idx_ref.shape[1]
    stars = pos_ref.shape[1]

    half = n // 2
    core = me % 2

    chip = me // 2
    partner = me + 1 - 2 * core
    lead = min(4, (half - 1) // 2 * 2)

    def same_core(order, sign):
        offset = sign * ((order + 1) // 2) * (2 * (order % 2) - 1)
        return 2 * lax.rem(chip + (offset + half) % half, half) + core

    barrier = pltpu.get_barrier_semaphore()

    for peer in [partner] + [same_core(order, 1) for order in range(1, half)]:
        pl.semaphore_signal(
            barrier, inc=1, device_id={"blk": peer}, device_id_type=pl.DeviceIdType.MESH
        )

    local_idx = idx_ref[...] - me * stars
    table = jnp.concatenate(
        [pos_ref[...], vel_ref[...], mass_ref[...], jnp.zeros((1, stars), F32)], axis=0
    )
    pieces = jnp.concatenate(split3(table), axis=0)
    picked = (lax.broadcasted_iota(jnp.int32, (stars, act), 0) == local_idx).astype(F32).astype(BF16)
    found = jnp.dot(pieces, picked, preferred_element_type=F32)
    own = found[0:8] + found[8:16] + found[16:24]
    mass_rows = own[6:8]

    pl.semaphore_wait(barrier, half)

    def copy_to(step, source, place, peer):
        return pltpu.make_async_remote_copy(
            src_ref=slots.at[step, source],
            dst_ref=slots.at[step, place],
            send_sem=send_sem.at[step, place],
            recv_sem=recv_sem.at[step, place],
            device_id={"blk": peer},
            device_id_type=pl.DeviceIdType.MESH,
        )

    def wait_at(step, place):
        copy_to(step, place, place, partner).wait_recv()

        @pl.when((place > 1) & (place <= half))
        def _():
            copy_to(step, place, place + half - 1, partner).start()

    row_id = lax.broadcasted_iota(jnp.int32, (8, act), 0)

    def add_pair(blocks, centre, fine):
        right = []
        for block in blocks:
            factor = jnp.where(row_id == 6, 1.0, block - centre)
            right.append(jnp.concatenate(split3(factor * block[6:7]), axis=0))
        right = jnp.concatenate(right + right if fine else right, axis=1)
        for top in range(0, act, ROWS):
            rows = slice(top, top + ROWS)
            highs, lows = [], []
            for block in blocks:
                for side in range(0, act, 128):
                    src = [block[c : c + 1, side : side + 128] for c in range(6)]
                    d = [src[c] - target[c, rows, :] for c in range(3)]
                    e = [src[c + 3] - target[c + 3, rows, :] for c in range(3)]
                    squared = d[0] * d[0] + d[1] * d[1] + d[2] * d[2] + 0.0025
                    radial = d[0] * e[0] + d[1] * e[1] + d[2] * e[2]
                    inverse = lax.rsqrt(squared)
                    inverse2 = inverse * inverse
                    w = inverse2 * inverse
                    both = jnp.concatenate([w, w * inverse2 * radial], axis=0)
                    high = both.astype(BF16)
                    highs.append(high)
                    if fine:
                        lows.append((both - high.astype(F32)).astype(BF16))
            total[2 * top : 2 * top + 2 * ROWS] += lax.dot_general(
                jnp.concatenate(highs + lows, axis=1),
                right,
                (((1,), (1,)), ((), ())),
                preferred_element_type=F32,
            )

    def field(step, own):
        fine = step == STEPS
        slots[step, 0] = own
        for order in range(half - 1, 0, -1):
            copy_to(step, 0, 1 + order, same_core(order, -1)).start()
        copy_to(step, 0, 1, partner).start()

        columns = own.T
        for c in range(6):
            target[c] = jnp.broadcast_to(columns[:, c : c + 1], (act, 128))
        centre = jnp.where(row_id[:, 0:1] < 6, jnp.mean(own, axis=1, keepdims=True), 0.0)
        total[...] = jnp.zeros_like(total)

        @pl.loop(0, n // 2)
        def _(pair):
            middle = (pair > lead // 2) & (pair < (n - lead) // 2)
            first = jnp.where(middle, half + pair - lead // 2, 2 * pair)
            second = jnp.where(middle, 1 + lead + pair - lead // 2, 2 * pair + 1)

            @pl.when(pair > 0)
            def _():
                wait_at(step, first)

            wait_at(step, second)
            add_pair([slots[step, first], slots[step, second]], centre, fine)

        sums = total[...].T
        sums = sums[0:8] + sums[8:16] + sums[16:24]
        tops = range(0, 2 * act, 2 * ROWS)
        plain = jnp.concatenate([sums[:, t : t + ROWS] for t in tops], axis=1)
        scaled = jnp.concatenate([sums[:, t + ROWS : t + 2 * ROWS] for t in tops], axis=1)
        about = own - centre
        accel = plain[0:3] - about[0:3] * plain[6:7]
        jerk = (
            plain[3:6]
            - about[3:6] * plain[6:7]
            - 3.0 * (scaled[0:3] - about[0:3] * scaled[6:7])
        )
        return accel, jerk

    pos, vel = own[0:3], own[3:6]
    accel, jerk = field(0, own)
    h = TIME_STEP
    for step in range(STEPS):
        pred_pos = pos + h * vel + h**2 / 2.0 * accel + h**3 / 6.0 * jerk
        pred_vel = vel + h * accel + h**2 / 2.0 * jerk
        accel_new, jerk_new = field(
            step + 1, jnp.concatenate([pred_pos, pred_vel, mass_rows], axis=0)
        )
        vel_new = vel + h / 2.0 * (accel + accel_new) + h**2 / 12.0 * (jerk - jerk_new)
        pos = pos + h / 2.0 * (vel + vel_new) + h**2 / 12.0 * (accel - accel_new)
        vel, accel, jerk = vel_new, accel_new, jerk_new
    out_ref[...] = jnp.concatenate([pos, vel, accel, jerk], axis=0)

    for step in range(STEPS + 1):

        @pl.loop(1, n)
        def _(place):
            copy_to(step, 0, place, partner).wait_send()


def solution(mesh):
    n = mesh.shape["blk"]

    def shards(positions, velocities, masses, active):
        act = active.shape[0]
        vmem = pl.BlockSpec(memory_space=pltpu.VMEM)
        packed = pl.pallas_call(
            functools.partial(kernel, n),
            out_shape=jax.ShapeDtypeStruct((12, act), F32),
            in_specs=[vmem] * 4,
            out_specs=vmem,
            scratch_shapes=[
                pltpu.VMEM((STEPS + 1, n, 8, act), F32),
                pltpu.VMEM((6, act, 128), F32),
                pltpu.VMEM((2 * act, 24), F32),
                pltpu.SemaphoreType.DMA((STEPS + 1, n)),
                pltpu.SemaphoreType.DMA((STEPS + 1, n)),
            ],
            compiler_params=pltpu.CompilerParams(collective_id=0, has_side_effects=True),
        )(positions, velocities, masses.reshape(1, -1), active.reshape(1, -1))
        return packed[0:3], packed[3:6], packed[6:9], packed[9:12]

    spec = P(None, ("clusters", "blk"))
    flat = P(("clusters", "blk"))
    return jax.shard_map(
        shards,
        mesh=mesh,
        in_specs=(spec, spec, flat, flat),
        out_specs=(spec, spec, spec, spec),
        check_vma=False,
    )
```

profile of v0, /device:TPU:0, one launch (start us, length us, event | category | flops | bytes accessed | tf_op | source)
XLA Modules:
  0.0 35.4 jit_solution(3779937095810559286)
XLA Ops:
  0.6 33.3 %shard_map.75 = f32[12,256]{1,0:T(8,128)} custom-call(f32[3,2048]{1,0:T(4,128)} %pos_ref.1, f32[3,2048]{1,0:T(4,128)} %vel_ref.1, f32[1,2048]{1,0:T(1,128)} %bitcast.2, s32[1,256]{1,0:T(1,128)} %bitcast.3), custom_call_target="tpu_custom_call" | custom-call | tf_op jit(solution)/shard_map/pallas_call | solution.py:189
  34.0 1.4 %fusion = (f32[3,256]{1,0:T(4,128)}, f32[3,256]{1,0:T(4,128)}, f32[3,256]{1,0:T(4,128)}, f32[3,256]{1,0:T(4,128)}) fusion(f32[12,256]{1,0:T(8,128)} %shard_map.75), kind=kLoop, calls=%fused_computation | loop fusion | bytes 24576 | tf_op jit(solution)/shard_map/slice | solution.py:203
where the time goes:
time: 35.6 us; the launch traced here: 35.4 us
  Pallas kernels  33.3 us (94%)
  local copies, waits for them, and re-layouts  1.42 us (4%)
  between operations  0.64 us (2%)
    pallas_call x1, Pallas kernels, shards(): pl.pallas_call(functools.partial(kernel, n), out_shape=jax.ShapeDtypeStru...  33.3 us
    slice x1, local copies, waits for them, and re-layouts, shards(): return (packed[0:3], packed[3:6], packed[6:9], packed[9:12])  1.42 us

commit v1 on v0

v1 whole, which is shorter than its diff:
```python
import functools

import jax
import jax.numpy as jnp
from jax import lax
from jax.experimental import pallas as pl
from jax.experimental.pallas import tpu as pltpu
from jax.sharding import PartitionSpec as P

STEPS = 2
TIME_STEP = 0.03125
ROWS = 32
SOFT = 0.0025
F32 = jnp.float32
BF16 = jnp.bfloat16


def split3(value):
    high = value.astype(BF16).astype(F32)
    rest = value - high
    middle = rest.astype(BF16).astype(F32)
    return high, middle, rest - middle


def kernel(
    n,
    pos_hbm,
    vel_hbm,
    mass_hbm,
    idx_hbm,
    out_ref,
    pos_ref,
    vel_ref,
    mass_ref,
    idx_ref,
    slots,
    target,
    feature,
    product,
    weights,
    right,
    total,
    in_sem,
    send_sem,
    recv_sem,
):
    me = lax.axis_index("blk")
    act = idx_ref.shape[1]
    stars = pos_ref.shape[1]

    half = n // 2
    chip = me // 2
    partner = me + 1 - 2 * lax.rem(me, 2)

    barrier = pltpu.get_barrier_semaphore()
    for k in range(1, n):
        pl.semaphore_signal(
            barrier,
            inc=1,
            device_id={"blk": lax.rem(me + k, n)},
            device_id_type=pl.DeviceIdType.MESH,
        )

    loads = [
        pltpu.make_async_copy(source, place, in_sem.at[k])
        for k, (source, place) in enumerate(
            [(idx_hbm, idx_ref), (pos_hbm, pos_ref), (vel_hbm, vel_ref), (mass_hbm, mass_ref)]
        )
    ]
    for load in loads:
        load.start()
    for load in loads:
        load.wait()

    row_id = lax.broadcasted_iota(jnp.int32, (8, act), 0)

    local_idx = idx_ref[...] - me * stars
    table = jnp.concatenate(
        [pos_ref[...], vel_ref[...], mass_ref[...], jnp.zeros((1, stars), F32)], axis=0
    )
    pieces = jnp.concatenate(split3(table), axis=0).astype(BF16)
    picked = (lax.broadcasted_iota(jnp.int32, (stars, act), 0) == local_idx).astype(F32).astype(BF16)
    found = jnp.dot(pieces, picked, preferred_element_type=F32)
    own = found[0:8] + found[8:16] + found[16:24]
    mass_rows = own[6:8]

    def chip_at(order):
        low = jnp.minimum(chip, half - 1 - chip)
        both = chip + ((order + 1) // 2) * (2 * lax.rem(order, 2) - 1)
        side = jnp.where(chip <= half - 1 - chip, order, half - 1 - order)
        return jnp.where(order <= 2 * low, both, side)

    def rows_at(step):
        return slice(0, 7 if step == 0 else 6)

    def send(step, peer):
        block = slots.at[step, me, rows_at(step)]
        return pltpu.make_async_remote_copy(
            src_ref=block,
            dst_ref=block,
            send_sem=send_sem.at[step],
            recv_sem=recv_sem.at[step, chip],
            device_id={"blk": peer},
            device_id_type=pl.DeviceIdType.MESH,
        )

    def arrival(step, first, count, source):
        blocks = slots.at[step, pl.ds(first, count), rows_at(step)]
        return pltpu.make_async_remote_copy(
            src_ref=blocks,
            dst_ref=blocks,
            send_sem=send_sem.at[step],
            recv_sem=recv_sem.at[step, source],
            device_id={"blk": partner},
            device_id_type=pl.DeviceIdType.MESH,
        )

    def dots(a, b):
        terms = a * b
        return terms[0:1] + terms[1:2] + terms[2:3]

    def stack(value, order, last):
        parts = split3(value)
        return jnp.concatenate([parts[k] for k in order] + [last, jnp.zeros_like(last)], axis=0)

    def prepare(step, source, centre, fine):
        for core in range(2):
            about = jnp.where(row_id < 6, slots[step, 2 * source + core] - centre, 0.0)
            factor = jnp.where(row_id == 6, 1.0, about)
            mass = slots[0, 2 * source + core, 6:7]
            right[core] = jnp.concatenate(split3(factor * mass), axis=0).astype(BF16)
            across = dots(about[0:3], about[3:6])
            square = dots(about[0:3], about[0:3])
            about = jnp.where(row_id == 6, across, jnp.where(row_id == 7, square, about))
            near = stack(about, (0, 0, 1, 1, 0, 2), jnp.ones_like(about)).astype(BF16)
            if fine:
                product[core, 0:act] = jnp.dot(
                    feature[act : 2 * act, :], near, preferred_element_type=F32
                )
            else:
                product[core] = jnp.dot(feature[...], near, preferred_element_type=F32)

    def weigh(step, source, fine):
        for core in range(2):
            for top in range(0, act, ROWS):
                rows = slice(top, top + ROWS)
                for side in range(0, act, 128):
                    lanes = slice(side, side + 128)
                    if fine:
                        d = [
                            slots[step, 2 * source + core, c : c + 1, lanes] - target[c, rows, :]
                            for c in range(3)
                        ]
                        squared = d[0] * d[0] + d[1] * d[1] + (d[2] * d[2] + SOFT)
                        radial = product[core, rows, lanes]
                    else:
                        squared = product[core, rows, lanes]
                        radial = product[core, act + top : act + top + ROWS, lanes]
                    inverse = lax.rsqrt(squared)
                    inverse2 = inverse * inverse
                    w = inverse2 * inverse
                    z = w * inverse2 * radial
                    for k, value in enumerate([w, z]):
                        high = value.astype(BF16)
                        weights[k, core, rows, lanes] = high
                        if fine:
                            low = (value - high.astype(F32)).astype(BF16)
                            weights[2 + k, core, rows, lanes] = low

    def reduce(fine):
        for core in range(2):
            for k in range(4 if fine else 2):
                total[k % 2] += lax.dot_general(
                    right[core],
                    weights[k, core],
                    (((1,), (1,)), ((), ())),
                    preferred_element_type=F32,
                )

    def field(step, own):
        fine = step == STEPS
        slots[step, me] = own
        if step == 0:
            pl.semaphore_wait(barrier, n - 1)
        send(step, partner).start()
        for order in range(1, half):
            there = 2 * chip_at(order)
            send(step, there).start()
            send(step, there + 1).start()

        centre = jnp.where(row_id[:, 0:1] < 6, jnp.mean(own, axis=1, keepdims=True), 0.0)
        about = own - centre
        none, one = jnp.zeros((1, act), F32), jnp.ones((1, act), F32)
        pad = jnp.zeros((5, act), F32)
        if fine:
            columns = own[0:8].T
            for c in range(3):
                target[c] = jnp.broadcast_to(columns[:, c : c + 1], (act, 128))
        else:
            square = dots(about[0:3], about[0:3]) + SOFT
            value = jnp.concatenate([-2.0 * about[0:3], none, none, none, none, one], axis=0)
            last = jnp.concatenate(list(split3(square)) + [pad], axis=0)
            feature[0:act, :] = stack(value, (0, 1, 0, 1, 2, 0), last).T.astype(BF16)
        across = dots(about[0:3], about[3:6])
        value = jnp.concatenate([-about[3:6], -about[0:3], one, none], axis=0)
        last = jnp.concatenate(list(split3(across)) + [pad], axis=0)
        feature[act : 2 * act, :] = stack(value, (0, 1, 0, 1, 2, 0), last).T.astype(BF16)
        total[...] = jnp.zeros_like(total)

        arrival(step, partner, 1, chip).wait_recv()
        prepare(step, chip, centre, fine)
        weigh(step, chip, fine)

        @pl.loop(1, half)
        def _(order):
            source = chip_at(order)
            arrival(step, 2 * source, 2, source).wait_recv()
            reduce(fine)
            prepare(step, source, centre, fine)
            weigh(step, source, fine)

        reduce(fine)
        plain, scaled = [total[k][0:8] + total[k][8:16] + total[k][16:24] for k in range(2)]
        accel = plain[0:3] - about[0:3] * plain[6:7]
        jerk = (
            plain[3:6]
            - about[3:6] * plain[6:7]
            - 3.0 * (scaled[0:3] - about[0:3] * scaled[6:7])
        )
        return accel, jerk

    pos, vel = own[0:3], own[3:6]
    accel, jerk = field(0, own)
    h = TIME_STEP
    for step in range(STEPS):
        pred_pos = pos + h * vel + h**2 / 2.0 * accel + h**3 / 6.0 * jerk
        pred_vel = vel + h * accel + h**2 / 2.0 * jerk
        accel_new, jerk_new = field(
            step + 1, jnp.concatenate([pred_pos, pred_vel, mass_rows], axis=0)
        )
        vel_new = vel + h / 2.0 * (accel + accel_new) + h**2 / 12.0 * (jerk - jerk_new)
        pos = pos + h / 2.0 * (vel + vel_new) + h**2 / 12.0 * (accel - accel_new)
        vel, accel, jerk = vel_new, accel_new, jerk_new
    out_ref[...] = jnp.concatenate([pos, vel, accel, jerk], axis=0)

    for step in range(STEPS + 1):
        arrival(step, 0, n - 1, 0).wait_send()


def solution(mesh):
    n = mesh.shape["blk"]

    def shards(positions, velocities, masses, active):
        act, stars = active.shape[0], masses.shape[0]
        hbm = pl.BlockSpec(memory_space=pltpu.HBM)
        packed = pl.pallas_call(
            functools.partial(kernel, n),
            out_shape=jax.ShapeDtypeStruct((12, act), F32),
            in_specs=[hbm] * 4,
            out_specs=pl.BlockSpec(memory_space=pltpu.VMEM),
            scratch_shapes=[
                pltpu.VMEM((3, stars), F32),
                pltpu.VMEM((3, stars), F32),
                pltpu.VMEM((1, stars), F32),
                pltpu.VMEM((1, act), jnp.int32),
                pltpu.VMEM((STEPS + 1, n, 8, act), F32),
                pltpu.VMEM((3, act, 128), F32),
                pltpu.VMEM((2 * act, 64), BF16),
                pltpu.VMEM((2, 2 * act, act), F32),
                pltpu.VMEM((4, 2, act, act), BF16),
                pltpu.VMEM((2, 24, act), BF16),
                pltpu.VMEM((2, 24, act), F32),
                pltpu.SemaphoreType.DMA((4,)),
                pltpu.SemaphoreType.DMA((STEPS + 1,)),
                pltpu.SemaphoreType.DMA((STEPS + 1, n // 2)),
            ],
            compiler_params=pltpu.CompilerParams(
                collective_id=0, has_side_effects=True, vmem_limit_bytes=24 * 1024 * 1024
            ),
        )(positions, velocities, masses.reshape(1, -1), active.reshape(1, -1))
        return packed[0:3], packed[3:6], packed[6:9], packed[9:12]

    spec = P(None, ("clusters", "blk"))
    flat = P(("clusters", "blk"))
    return jax.shard_map(
        shards,
        mesh=mesh,
        in_specs=(spec, spec, flat, flat),
        out_specs=(spec, spec, spec, spec),
        check_vma=False,
    )
```

time: 35.6 us -> 30.2 us (0.85)
  Pallas kernels: 33.3 us -> 25.7 us
  local copies, waits for them, and re-layouts: 1.42 us -> 3.49 us
    pallas_call x1, Pallas kernels: 33.3 us -> 25.7 us  [shards(): pl.pallas_call(functools.partial(kernel, n), out_shape=jax.ShapeDtypeStru...]
    unnamed x0 -> x8, local copies, waits for them, and re-layouts: none -> 2.88 us
    slice x1, local copies, waits for them, and re-layouts: 1.42 us -> 0.61 us  [shards(): return (packed[0:3], packed[3:6], packed[6:9], packed[9:12])]
where the time goes in v1:
time: 30.2 us; the launch traced here: 29.9 us
  Pallas kernels  25.7 us (85%)
  local copies, waits for them, and re-layouts  3.49 us (12%)
  between operations  0.65 us (2%)
    pallas_call x1, Pallas kernels, shards(): pl.pallas_call(functools.partial(kernel, n), out_shape=jax.ShapeDtypeStru...  25.7 us
    unnamed x8, local copies, waits for them, and re-layouts  2.88 us
    slice x1, local copies, waits for them, and re-layouts, shards(): return (packed[0:3], packed[3:6], packed[6:9], packed[9:12])  0.61 us

profile of v1, /device:TPU:0, one launch (start us, length us, event | category | flops | bytes accessed | tf_op | source)
XLA Modules:
  0.0 29.9 jit_solution(16854510175440740447)
XLA Ops:
  0.6 0.0 copy-start.3
  0.6 0.7 %copy-done.3 = s32[256]{0:T(256)S(1)} copy-done((s32[256]{0:T(256)S(1)}, s32[256]{0:T(256)}, u32[]{:S(2)}) %copy-start.3) | copy-done | bytes 1048
  1.3 0.0 copy-start
  1.3 0.8 %copy-done = f32[3,2048]{1,0:T(4,128)S(1)} copy-done((f32[3,2048]{1,0:T(4,128)S(1)}, f32[3,2048]{1,0:T(4,128)}, u32[]{:S(2)}) %copy-start) | copy-done | bytes 24600
  2.1 0.0 copy-start.1
  2.1 0.8 %copy-done.1 = f32[3,2048]{1,0:T(4,128)S(1)} copy-done((f32[3,2048]{1,0:T(4,128)S(1)}, f32[3,2048]{1,0:T(4,128)}, u32[]{:S(2)}) %copy-start.1) | copy-done | bytes 24600
  2.8 0.0 copy-start.2
  2.8 0.7 %copy-done.2 = f32[2048]{0:T(1024)S(1)} copy-done((f32[2048]{0:T(1024)S(1)}, f32[2048]{0:T(1024)}, u32[]{:S(2)}) %copy-start.2) | copy-done | bytes 8216
  3.5 25.7 %shard_map.75 = f32[12,256]{1,0:T(8,128)S(1)} custom-call(f32[3,2048]{1,0:T(4,128)S(1)} %copy-done, f32[3,2048]{1,0:T(4,128)S(1)} %copy-done.1, f32[1,2048]{1,0:T(1,128)S(1)} %bitcast.2, s32[1,256]{1,0:T(1,128)S(1)} %bitcast.3), custom_call_target="tpu_custom_call" | custom-call | tf_op jit(solution)/shard_map/pallas_call | solution.py:256
  29.3 0.6 %fusion = (f32[3,256]{1,0:T(4,128)}, f32[3,256]{1,0:T(4,128)}, f32[3,256]{1,0:T(4,128)}, f32[3,256]{1,0:T(4,128)}) fusion(f32[12,256]{1,0:T(8,128)S(1)} %shard_map.75), kind=kLoop, calls=%fused_computation | loop fusion | bytes 24576 | tf_op jit(solution)/shard_map/slice | solution.py:281
Async XLA Ops:
  0.6 0.7 %copy-start.3 = (s32[256]{0:T(256)S(1)}, s32[256]{0:T(256)}, u32[]{:S(2)}) copy-start(s32[256]{0:T(256)} %param.7) | copy-start | bytes 3076
  1.3 0.8 %copy-start = (f32[3,2048]{1,0:T(4,128)S(1)}, f32[3,2048]{1,0:T(4,128)}, u32[]{:S(2)}) copy-start(f32[3,2048]{1,0:T(4,128)} %pos_hbm.1) | copy-start | bytes 73732
  2.1 0.8 %copy-start.1 = (f32[3,2048]{1,0:T(4,128)S(1)}, f32[3,2048]{1,0:T(4,128)}, u32[]{:S(2)}) copy-start(f32[3,2048]{1,0:T(4,128)} %vel_hbm.1) | copy-start | bytes 73732
  2.8 0.7 %copy-start.2 = (f32[2048]{0:T(1024)S(1)}, f32[2048]{0:T(1024)}, u32[]{:S(2)}) copy-start(f32[2048]{0:T(1024)} %param.6) | copy-start | bytes 24580

commit v2 on v1

--- a/solution.py
+++ b/solution.py
@@ -35,6 +35,7 @@
     idx_ref,
     slots,
     target,
+    across_rows,
     feature,
     product,
     weights,
@@ -121,59 +122,61 @@
 
     def stack(value, order, last):
         parts = split3(value)
-        return jnp.concatenate([parts[k] for k in order] + [last, jnp.zeros_like(last)], axis=0)
+        return jnp.concatenate([parts[k] for k in order] + last, axis=0)
 
     def prepare(step, source, centre, fine):
-        for core in range(2):
-            about = jnp.where(row_id < 6, slots[step, 2 * source + core] - centre, 0.0)
+        for side in range(2):
+            about = jnp.where(row_id < 6, slots[step, 2 * source + side] - centre, 0.0)
             factor = jnp.where(row_id == 6, 1.0, about)
-            mass = slots[0, 2 * source + core, 6:7]
-            right[core] = jnp.concatenate(split3(factor * mass), axis=0).astype(BF16)
+            mass = slots[0, 2 * source + side, 6:7]
+            right[side] = jnp.concatenate(split3(factor * mass), axis=0).astype(BF16)
             across = dots(about[0:3], about[3:6])
             square = dots(about[0:3], about[0:3])
             about = jnp.where(row_id == 6, across, jnp.where(row_id == 7, square, about))
-            near = stack(about, (0, 0, 1, 1, 0, 2), jnp.ones_like(about)).astype(BF16)
+            near = stack(about, (0, 0, 1, 1, 0, 2), [jnp.ones_like(about), jnp.zeros_like(about)])
             if fine:
-                product[core, 0:act] = jnp.dot(
-                    feature[act : 2 * act, :], near, preferred_element_type=F32
+                product[side, :, 0:act] = jnp.dot(
+                    across_rows[...], near.astype(BF16), preferred_element_type=F32
                 )
             else:
-                product[core] = jnp.dot(feature[...], near, preferred_element_type=F32)
+                product[side] = jnp.dot(
+                    near.T.astype(BF16), feature[...], preferred_element_type=F32
+                )
 
     def weigh(step, source, fine):
-        for core in range(2):
+        for side in range(2):
             for top in range(0, act, ROWS):
                 rows = slice(top, top + ROWS)
-                for side in range(0, act, 128):
-                    lanes = slice(side, side + 128)
+                for left in range(0, act, 128):
+                    lanes = slice(left, left + 128)
                     if fine:
                         d = [
-                            slots[step, 2 * source + core, c : c + 1, lanes] - target[c, rows, :]
+                            slots[step, 2 * source + side, c : c + 1, lanes] - target[c, rows, :]
                             for c in range(3)
                         ]
                         squared = d[0] * d[0] + d[1] * d[1] + (d[2] * d[2] + SOFT)
-                        radial = product[core, rows, lanes]
+                        radial = product[side, rows, lanes]
                     else:
-                        squared = product[core, rows, lanes]
-                        radial = product[core, act + top : act + top + ROWS, lanes]
+                        squared = product[side, rows, lanes]
+                        radial = product[side, rows, act + left : act + left + 128]
                     inverse = lax.rsqrt(squared)
                     inverse2 = inverse * inverse
                     w = inverse2 * inverse
                     z = w * inverse2 * radial
                     for k, value in enumerate([w, z]):
                         high = value.astype(BF16)
-                        weights[k, core, rows, lanes] = high
+                        weights[k, side, rows, lanes] = high
                         if fine:
                             low = (value - high.astype(F32)).astype(BF16)
-                            weights[2 + k, core, rows, lanes] = low
+                            weights[2 + k, side, rows, lanes] = low
 
     def reduce(fine):
-        for core in range(2):
+        for side in range(2):
             for k in range(4 if fine else 2):
                 total[k % 2] += lax.dot_general(
-                    right[core],
-                    weights[k, core],
-                    (((1,), (1,)), ((), ())),
+                    right[side],
+                    weights[k, side],
+                    (((1,), (1 if fine else 0,)), ((), ())),
                     preferred_element_type=F32,
                 )
 
@@ -191,20 +194,22 @@
         centre = jnp.where(row_id[:, 0:1] < 6, jnp.mean(own, axis=1, keepdims=True), 0.0)
         about = own - centre
         none, one = jnp.zeros((1, act), F32), jnp.ones((1, act), F32)
-        pad = jnp.zeros((5, act), F32)
+        pad = jnp.zeros((13, act), F32)
+        if not fine:
+            square = dots(about[0:3], about[0:3]) + SOFT
+            value = jnp.concatenate([-2.0 * about[0:3], none, none, none, none, one], axis=0)
+            last = [*split3(square), pad]
+            feature[:, 0:act] = stack(value, (0, 1, 0, 1, 2, 0), last).astype(BF16)
+        across = dots(about[0:3], about[3:6])
+        value = jnp.concatenate([-about[3:6], -about[0:3], one, none], axis=0)
+        last = [*split3(across), pad]
         if fine:
-            columns = own[0:8].T
+            across_rows[...] = stack(value, (0, 1, 0, 1, 2, 0), last).T.astype(BF16)
+            columns = own.T
             for c in range(3):
                 target[c] = jnp.broadcast_to(columns[:, c : c + 1], (act, 128))
         else:
-            square = dots(about[0:3], about[0:3]) + SOFT
-            value = jnp.concatenate([-2.0 * about[0:3], none, none, none, none, one], axis=0)
-            last = jnp.concatenate(list(split3(square)) + [pad], axis=0)
-            feature[0:act, :] = stack(value, (0, 1, 0, 1, 2, 0), last).T.astype(BF16)
-        across = dots(about[0:3], about[3:6])
-        value = jnp.concatenate([-about[3:6], -about[0:3], one, none], axis=0)
-        last = jnp.concatenate(list(split3(across)) + [pad], axis=0)
-        feature[act : 2 * act, :] = stack(value, (0, 1, 0, 1, 2, 0), last).T.astype(BF16)
+            feature[:, act : 2 * act] = stack(value, (0, 1, 0, 1, 2, 0), last).astype(BF16)
         total[...] = jnp.zeros_like(total)
 
         arrival(step, partner, 1, chip).wait_recv()
@@ -253,6 +258,10 @@
     def shards(positions, velocities, masses, active):
         act, stars = active.shape[0], masses.shape[0]
         hbm = pl.BlockSpec(memory_space=pltpu.HBM)
+        positions, velocities, masses, active = [
+            pltpu.with_memory_space_constraint(value, pltpu.HBM)
+            for value in (positions, velocities, masses.reshape(1, -1), active.reshape(1, -1))
+        ]
         packed = pl.pallas_call(
             functools.partial(kernel, n),
             out_shape=jax.ShapeDtypeStruct((12, act), F32),
@@ -265,8 +274,9 @@
                 pltpu.VMEM((1, act), jnp.int32),
                 pltpu.VMEM((STEPS + 1, n, 8, act), F32),
                 pltpu.VMEM((3, act, 128), F32),
-                pltpu.VMEM((2 * act, 64), BF16),
-                pltpu.VMEM((2, 2 * act, act), F32),
+                pltpu.VMEM((act, 64), BF16),
+                pltpu.VMEM((64, 2 * act), BF16),
+                pltpu.VMEM((2, act, 2 * act), F32),
                 pltpu.VMEM((4, 2, act, act), BF16),
                 pltpu.VMEM((2, 24, act), BF16),
                 pltpu.VMEM((2, 24, act), F32),
@@ -277,7 +287,7 @@
             compiler_params=pltpu.CompilerParams(
                 collective_id=0, has_side_effects=True, vmem_limit_bytes=24 * 1024 * 1024
             ),
-        )(positions, velocities, masses.reshape(1, -1), active.reshape(1, -1))
+        )(positions, velocities, masses, active)
         return packed[0:3], packed[3:6], packed[6:9], packed[9:12]
 
     spec = P(None, ("clusters", "blk"))

time: 30.2 us -> 26.8 us (0.89)
  local copies, waits for them, and re-layouts: 3.49 us -> 0.61 us
    unnamed x8 -> x0, local copies, waits for them, and re-layouts: 2.88 us -> none
    pallas_call x1, Pallas kernels: 25.7 us -> 25.4 us  [shards(): pl.pallas_call(functools.partial(kernel, n), out_shape=jax.ShapeDtypeStru...]
where the time goes in v2:
time: 26.8 us; the launch traced here: 26.6 us
  Pallas kernels  25.4 us (95%)
  between operations  0.64 us (2%)
  local copies, waits for them, and re-layouts  0.61 us (2%)
    pallas_call x1, Pallas kernels, shards(): pl.pallas_call(functools.partial(kernel, n), out_shape=jax.ShapeDtypeStru...  25.4 us
    slice x1, local copies, waits for them, and re-layouts, shards(): return (packed[0:3], packed[3:6], packed[6:9], packed[9:12])  0.61 us

profile of v2, /device:TPU:0, one launch (start us, length us, event | category | flops | bytes accessed | tf_op | source)
XLA Modules:
  0.0 26.6 jit_solution(8728777196006473054)
XLA Ops:
  0.6 25.4 %shard_map.75 = f32[12,256]{1,0:T(8,128)S(1)} custom-call(f32[3,2048]{1,0:T(4,128)} %pos_hbm.1, f32[3,2048]{1,0:T(4,128)} %vel_hbm.1, f32[1,2048]{1,0:T(1,128)} %bitcast.2, s32[1,256]{1,0:T(1,128)} %bitcast.3), custom_call_target="tpu_custom_call" | custom-call | tf_op jit(solution)/shard_map/pallas_call | solution.py:265
  26.0 0.6 %fusion = (f32[3,256]{1,0:T(4,128)}, f32[3,256]{1,0:T(4,128)}, f32[3,256]{1,0:T(4,128)}, f32[3,256]{1,0:T(4,128)}) fusion(f32[12,256]{1,0:T(8,128)S(1)} %shard_map.75), kind=kLoop, calls=%fused_computation | loop fusion | bytes 24576 | tf_op jit(solution)/shard_map/slice | solution.py:291
